TPU v7x, 32 devices: a whole 2x2x4 slice. The times are simulated.
32 devices in a mesh: tp: 4 (over z), dp: 8 (over y, x, core).
Axes of the slice: x: 2, y: 2, z: 4, core: 2. Of those that a mesh axis runs over, the one named last changes fastest.
Arguments:
- w_query: bfloat16 [16, 1024, 1024], P(None, ('dp', 'tp'))
- w_key: bfloat16 [16, 1024, 1024], P(None, ('dp', 'tp'))
- w_value: bfloat16 [16, 1024, 1024], P(None, ('dp', 'tp'))
- w_out: bfloat16 [16, 1024, 1024], P(None, ('dp', 'tp'))
- w_gate: bfloat16 [16, 1024, 2816], P(None, ('dp', 'tp'))
- w_up: bfloat16 [16, 1024, 2816], P(None, ('dp', 'tp'))
- w_down: bfloat16 [16, 2816, 1024], P(None, ('dp', 'tp'))
- w_head: bfloat16 [1024, 151936], P(('dp', 'tp'))
Outputs:
- output 1: bfloat16 [16, 3072, 1024], P(None, 'tp')
- output 2: bfloat16 [16, 1024, 1024], P(None, None, 'tp')
- output 3: bfloat16 [16, 5632, 1024], P(None, 'tp')
- output 4: bfloat16 [16, 1024, 2816], P(None, None, 'tp')
- output 5: bfloat16 [151936, 1024], P('tp')
All inputs are finite; a program needn't handle non-finite values.
Results may differ from a plain program's by a relative error of at most 0.001.
Values are sent between devices in bfloat16 or wider.
A program may use at most 1 GiB of HBM per device.

v0:
```python
import functools

import jax
import jax.numpy as jnp
from jax import lax
from jax.experimental import pallas as pl
from jax.experimental.pallas import tpu as pltpu
from jax.sharding import PartitionSpec as P


MESH = pl.DeviceIdType.MESH
LANES = 128
VMEM = 67_000_000
AHEAD = 14
BUFFERS = 6
LAG = 1
SHARE_AT = 20
SLOTS = 8
COUNTED = 4
WHOLE = 3
WHOLE_AT = 2
RANKS_AT = 10
PARTS = 4
GROUP = 4


class Plan:
    def __init__(self, tp, dp, w_query, w_gate, w_out, w_down, w_head):
        self.tp, self.dp = tp, dp
        self.layers, self.rows, columns = w_query.shape
        self.part = columns // tp
        self.wide = w_gate.shape[2] // tp
        self.vocab = w_head.shape[1] // tp
        self.head_tiles = w_head.shape[1] // LANES
        self.chunk = 3 * self.part + 2 * self.wide
        self.wide_window = -(-self.wide // LANES) * LANES
        self.layer_window = 3 * self.part + 2 * self.wide_window
        self.head_chunks = -(-self.vocab // self.chunk)
        self.chunks = self.layers + self.head_chunks
        end = self.vocab - (self.head_chunks - 1) * self.chunk
        self.tail_window = -(-(end + LANES) // LANES) * LANES
        self.window_tiles = (self.head_chunks - 1) * self.chunk // LANES + self.tail_window // LANES
        self.shift = max(self.vocab * r - self.head_base(r) * LANES for r in range(tp))
        self.out_rows, self.down_rows = w_out.shape[1], w_down.shape[1]
        self.downs, self.outs = 2 * tp * self.down_rows, 2 * tp * self.out_rows
        self.piece = self.downs + self.outs
        self.share = self.layers // dp
        self.columns = w_out.shape[2]
        self.whole = WHOLE * LANES
        self.cut = self.columns - self.whole
        self.extra_first = self.vocab - self.share * WHOLE * self.piece
        self.ring = self.layers + self.extra_first // self.chunk
        self.tail = self.extra_first % self.chunk
        self.counts = -(-self.ring // COUNTED) + 1

    def wide_base(self, rank):
        return (self.wide * rank) // LANES

    def head_base(self, rank):
        base = (self.vocab * rank) // LANES
        return base - (rank // (self.tp - 1)) * (self.vocab * (self.tp - 1) // LANES + self.window_tiles - self.head_tiles)


def gather_kernel(plan, q, k, v, o, g, u, d, h, slabs, own_0, own_1, whole, stop_0, stop_1, land_d, land_o, zbuf, tbuf,
                  z_recv, z_send, local, x_recv, y_recv, a_recv, b_recv, pair_recv, send, stop_recv, share_recv,
                  share_send, land_recv, land_send, whole_recv, whole_send, whole_pair_recv, whole_pair_send,
                  keep_d, keep_o, keep_sem, packed, pack_sem):
    z, dp = lax.axis_index("tp"), lax.axis_index("dp")
    core, x, y = dp % 2, (dp // 2) % 2, dp // 4
    x_peer = y * 4 + (1 - x) * 2 + core
    y_peer = (1 - y) * 4 + x * 2 + core
    diagonal = (1 - y) * 4 + (1 - x) * 2 + core
    pair = dp + 1 - 2 * core
    rows, chunk, tail = plan.rows, plan.chunk, plan.tail
    layers, ring, last = plan.layers, plan.ring, plan.chunks - 1
    my_rows = pl.ds(pl.multiple_of(z * rows, rows), rows)

    def lanes(first_tile, width):
        return pl.ds(pl.multiple_of(first_tile * LANES, LANES), width)

    def remote(source, target, send_sem, recv_sem, **to):
        pltpu.make_async_remote_copy(source, target, send_sem, recv_sem, device_id=to, device_id_type=MESH).start()

    def wait_for(ref, sem):
        pltpu.make_async_copy(ref, ref, sem).wait()


    def z_slot(index):
        return index - layers + layers // GROUP

    def rank_at(step):
        return (z + step + core * (plan.tp - 2 * step)) % plan.tp

    def layer_pieces(first, rank):
        some, part, wide = pl.ds(first, GROUP), plan.part, plan.wide_window
        narrow = lanes(rank * (part // LANES), part)
        window = lanes(plan.wide_base(rank), wide)
        return [
            (q.at[some, :, narrow], 0, part),
            (k.at[some, :, narrow], part, part),
            (v.at[some, :, narrow], 2 * part, part),
            (g.at[some, :, window], 3 * part, wide),
            (u.at[some, :, window], 3 * part + wide, wide),
        ]

    def collect(group):
        for step in range(1, plan.tp):
            for source, column, width in layer_pieces(group * GROUP, rank_at(step)):
                target = packed.at[group, step - 1, :, :, pl.ds(column, width)]
                pltpu.make_async_copy(source, target, pack_sem.at[group]).start()
        for source, column, width in layer_pieces(group * GROUP, z):
            target = zbuf.at[pl.ds(group * GROUP, GROUP), my_rows, pl.ds(column, width)]
            pltpu.make_async_copy(source, target, z_recv.at[group]).start()

    def exchange_layers(group):
        wait_for(packed.at[group], pack_sem.at[group])
        for step in range(1, plan.tp):
            index = group * GROUP
            target = zbuf.at[pl.ds(index, GROUP), my_rows, :]
            remote(packed.at[group, step - 1], target, z_send.at[0], z_recv.at[group], tp=rank_at(step))

    def exchange_head(index, width):
        def piece(rank):
            return h.at[:, lanes(plan.head_base(rank) + (index - layers) * (chunk // LANES), width)]

        target = zbuf.at[index, my_rows, pl.ds(0, width)]
        sent = z_send.at[1 if width == chunk else 2]
        for step in range(1, plan.tp):
            remote(piece(rank_at(step)), target, sent, z_recv.at[z_slot(index)], tp=rank_at(step))
        pltpu.make_async_copy(piece(z), target, z_recv.at[z_slot(index)]).start()

    def start_exchange(index):
        @pl.when((index >= layers) & (index < last))
        def _():
            exchange_head(index, chunk)

        @pl.when(index == last)
        def _():
            exchange_head(last, plan.tail_window)

    def wait_exchange(index, width):
        wait_for(zbuf.at[index, :, pl.ds(0, width)], z_recv.at[z_slot(index)])


    def turn(slot, tile, index, source_tile):
        tbuf[slot, pl.ds(tile * LANES, LANES), :] = zbuf[index, :, pl.ds(source_tile * LANES, LANES)].T

    def store(slot, first, index, to, count):
        pltpu.make_async_copy(
            tbuf.at[slot, pl.ds(first, count), :], slabs.at[dp, index, pl.ds(to, count), :], local.at[slot]
        ).start()

    def make_layer(index, slot):
        @pl.when(index % GROUP == 0)
        def _():
            wait_for(zbuf.at[pl.ds(index, GROUP), :, pl.ds(0, plan.layer_window)], z_recv.at[index // GROUP])

        for tile in range(plan.layer_window // LANES):
            turn(slot, tile, index, tile)
        shift = plan.wide * z - plan.wide_base(z) * LANES
        narrow, wide, window = 3 * plan.part, plan.wide, plan.wide_window
        store(slot, 0, index, 0, narrow)
        store(slot, pl.multiple_of(narrow + shift, 16), index, narrow, wide)
        store(slot, pl.multiple_of(narrow + window + shift, 16), index, narrow + wide, wide)

    head_shift = plan.vocab * z - plan.head_base(z) * LANES

    def make_head(index, slot):
        @pl.when(index == layers)
        def _():
            wait_exchange(index, chunk)

        wait_exchange(index + 1, chunk)
        tiles = chunk // LANES
        for tile in range(tiles):
            turn(slot, tile, index, tile)
        for tile in range(2):
            turn(slot, tiles + tile, index + 1, tile)
        store(slot, pl.multiple_of(head_shift, 16), index, 0, chunk)

    def turn_rows(slot, first, count):
        start = first // LANES
        for tile in range(-(-(first % LANES + plan.shift + count) // LANES)):
            at = start + tile
            turn(slot, tile, layers + at // (chunk // LANES), at % (chunk // LANES))
        return pl.multiple_of(first % LANES + head_shift, 16)

    def make_tail(slot):
        wait_exchange(ring + 1, chunk)
        store(slot, turn_rows(slot, (ring - layers) * chunk, tail), ring, 0, tail)

    def make_extra():
        for index in range(ring + 2, last):
            wait_exchange(index, chunk)
        wait_exchange(last, plan.tail_window)
        blocks = plan.share * WHOLE

        def stored(n, own):
            wait_for(own.at[:, pl.ds(plan.cut, LANES)], local.at[n % 2])

        for n in range(blocks):
            own = (own_0, own_1)[n // WHOLE]
            if n >= 2:
                stored(n, own)
            at = turn_rows(n % 2, plan.extra_first + n * plan.piece, plan.piece)
            pltpu.make_async_copy(
                tbuf.at[n % 2, pl.ds(at, plan.piece), :],
                own.at[:, pl.ds(plan.cut + n % WHOLE * LANES, LANES)], local.at[n % 2],
            ).start()
        for n in range(blocks - min(2, blocks), blocks):
            stored(n, own_0)


    def slab_view(index):
        return lambda owner, first, count: slabs.at[owner, index, pl.ds(first, count), :]

    def push(part, index, recv, to):
        remote(part, part, send.at[counted(index)], recv.at[index % SLOTS], dp=to)

    def push_pair(part, index):
        remote(part, part, send.at[counted(index)], pair_recv.at[counted(index)], dp=pair)

    def counted(index):
        return plan.counts - 1 if index is ring else index // COUNTED

    def send_own(view, index, slot, count):
        own = view(dp, 0, count)
        wait_for(own, local.at[slot])
        push(own, index, x_recv, x_peer)
        push(own, index, y_recv, y_peer)
        push_pair(own, index)

    def forward(view, index, count):
        half = count // 2
        slot = index % SLOTS
        wait_for(view(x_peer, 0, count), x_recv.at[slot])
        push(view(x_peer, half, half), index, b_recv, y_peer)
        push_pair(view(x_peer, 0, count), index)
        wait_for(view(y_peer, 0, count), y_recv.at[slot])
        push(view(y_peer, 0, half), index, a_recv, x_peer)
        push_pair(view(y_peer, 0, count), index)

    def forward_diagonal(view, index, count):
        half = count // 2
        slot = index % SLOTS
        wait_for(view(diagonal, 0, half), a_recv.at[slot])
        wait_for(view(diagonal, half, half), b_recv.at[slot])
        push_pair(view(diagonal, 0, count), index)

    def finish(index, some, count):
        wait_for(slabs.at[pl.ds(0, 7), some, pl.ds(0, count), :], send.at[index])
        wait_for(slabs.at[pl.ds(0, 4), some, pl.ds(0, count), :], pair_recv.at[index])


    def pieces(source_dp, to, place):
        all_rows = plan.downs
        downs = pl.ds(pl.multiple_of(place * plan.down_rows, 8), plan.down_rows)
        outs = pl.ds(pl.multiple_of(all_rows + place * plan.out_rows, 8), plan.out_rows)
        stop_downs, stop_outs = pl.ds(0, plan.down_rows), pl.ds(plan.down_rows, plan.out_rows)
        cut, home = pl.ds(plan.whole, plan.cut), pl.ds(0, plan.cut)
        found = []
        for n, (stop, own) in enumerate(((stop_0, own_0), (stop_1, own_1))):
            layer = to * 2 + n
            found.append((d.at[layer, :, cut], stop.at[source_dp, stop_downs, :], own.at[downs, home], n))
            found.append((o.at[layer, :, cut], stop.at[source_dp, stop_outs, :], own.at[outs, home], n))
        return found

    my_rank = dp // 2
    my_place = (dp % 2) * plan.tp + z
    stays = my_rank == z

    def share_in_plane():
        for step in range(1, plan.dp):
            to = (dp + step) % plan.dp

            @pl.when(stays)
            def _(to=to):
                for part, _, final, n in pieces(dp, to, my_place):
                    remote(part, final, share_send.at[n], share_recv.at[n], dp=to)

            @pl.when(jnp.logical_not(stays))
            def _(to=to):
                for part, stop, _, n in pieces(dp, to, my_place):
                    remote(part, stop, share_send.at[n], stop_recv.at[n, dp], dp=to)

        @pl.when(stays)
        def _():
            for part, _, final, n in pieces(dp, dp, my_place):
                pltpu.make_async_copy(part, final, share_recv.at[n]).start()

    def share_to_rank(source_dp):
        rank, place = source_dp // 2, (source_dp % 2) * plan.tp + z

        @pl.when((rank != z) & (source_dp == dp))
        def _():
            for part, _, final, n in pieces(dp, dp, place):
                remote(part, final, share_send.at[n], share_recv.at[n], tp=rank)

        @pl.when((rank != z) & (source_dp != dp))
        def _():
            for n, stop in enumerate((stop_0, stop_1)):
                wait_for(stop.at[source_dp], stop_recv.at[n, source_dp])
            for _, stop, final, n in pieces(source_dp, dp, place):
                remote(stop, final, share_send.at[n], share_recv.at[n], tp=rank)


    whole_columns = pl.ds(0, plan.whole)
    keep = (keep_d, keep_o)
    mine = ((d, land_d, plan.down_rows, 0), (o, land_o, plan.out_rows, plan.downs))
    half = layers // 2

    def whole_home(n, row):
        _, _, count, first = mine[n]
        return pl.ds(pl.multiple_of(first + row * count, 8), count)

    def landing(rank, some, act):
        pl.when(rank == z)(lambda: act([whole.at[some, whole_home(n, core * plan.tp + z), :] for n in range(2)]))
        pl.when(rank != z)(lambda: act([land.at[rank, some] for _, land, _, _ in mine]))

    every = pl.ds(0, layers)

    def whole_out():
        def act(places):
            for n, (source, _, _, _) in enumerate(mine):
                for to, at in ((x_peer, 0), (y_peer, 2)):
                    remote(source.at[:, :, whole_columns], places[n], land_send.at[n], land_recv.at[at + n], dp=to)

        landing(my_rank, every, act)

        @pl.when(stays)
        def _():
            for n, (source, _, _, _) in enumerate(mine):
                pltpu.make_async_copy(source.at[:, :, whole_columns], keep[n], keep_sem.at[n]).start()

    def whole_keep():
        @pl.when(stays)
        def _():
            for n in range(2):
                wait_for(keep[n], keep_sem.at[n])
                target = whole.at[:, whole_home(n, core * plan.tp + z), :]
                pltpu.make_async_copy(keep[n], target, keep_sem.at[2 + n]).start()

    def whole_forward():
        for owner, at, first, to, then in ((x_peer, 0, half, y_peer, 6), (y_peer, 2, 0, x_peer, 4)):
            def arrived(places, at=at):
                for n in range(2):
                    wait_for(places[n], land_recv.at[at + n])

            def on(places, to=to, then=then):
                for n in range(2):
                    remote(places[n], places[n], land_send.at[n], land_recv.at[then + n], dp=to)

            landing(owner // 2, every, arrived)
            landing(owner // 2, pl.ds(first, half), on)

    def whole_arrive():
        for first, at in ((0, 4), (half, 6)):
            def arrived(places, at=at):
                for n in range(2):
                    wait_for(places[n], land_recv.at[at + n])

            landing(diagonal // 2, pl.ds(first, half), arrived)

    def whole_to_rank(shift, part):
        rank = (z + shift + core * (plan.tp - 2 * shift)) % plan.tp
        some = pl.ds(part * (layers // PARTS), layers // PARTS)

        def move(sources):
            for n, source in enumerate(sources):
                target = whole.at[some, whole_home(n, core * plan.tp + z), :]
                remote(source, target, whole_send.at[n], whole_recv.at[n], tp=rank)

        pl.when(rank == my_rank)(lambda: move([source.at[some, :, whole_columns] for source, _, _, _ in mine]))
        pl.when(rank != my_rank)(lambda: move([land.at[rank, some] for _, land, _, _ in mine]))

    def whole_rows(which):
        return [
            whole.at[:, pl.ds(pl.multiple_of(first + which * plan.tp * count, 8), plan.tp * count), :]
            for _, _, count, first in mine
        ]

    def whole_to_pair():
        for n, part in enumerate(whole_rows(core)):
            away = pl.ds(0, (plan.tp - 1) * mine[n][2])
            wait_for(whole.at[:, away, :], whole_recv.at[n])

            @pl.when(stays)
            def _(n=n):
                wait_for(keep[n], keep_sem.at[2 + n])

            remote(part, part, whole_pair_send.at[n], whole_pair_recv.at[n], dp=pair)

    def whole_finish():
        for n, (_, land, count, first) in enumerate(mine):
            wait_for(land.at[pl.ds(0, 3)], land_send.at[n])
            wait_for(whole.at[:, pl.ds(first, (plan.tp - 1) * count), :], whole_send.at[n])
            wait_for(whole_rows(core)[n], whole_pair_send.at[n])
            wait_for(whole_rows(1 - core)[n], whole_pair_recv.at[n])

    groups = layers // GROUP
    barrier = pltpu.get_barrier_semaphore()
    peers = [{"tp": (z + step) % plan.tp} for step in range(1, plan.tp)]
    peers += [{"dp": (dp + step) % plan.dp} for step in range(1, plan.dp)]
    for peer in peers:
        pl.semaphore_signal(barrier, inc=1, device_id=peer, device_id_type=MESH)
    for group in range(groups):
        collect(group)
    pl.semaphore_wait(barrier, len(peers))

    whole_out()
    exchange_layers(0)
    share_in_plane()
    for group in range(1, groups):
        exchange_layers(group)
    for index in range(layers, AHEAD):
        start_exchange(index)

    def step(index, _):
        slot = index % 2

        @pl.when(index + AHEAD < plan.chunks)
        def _():
            start_exchange(index + AHEAD)

        @pl.when((index >= SHARE_AT) & (index < SHARE_AT + plan.dp))
        def _():
            share_to_rank(index - SHARE_AT)

        @pl.when(index == WHOLE_AT)
        def _():
            whole_keep()
            whole_forward()

        @pl.when(index == WHOLE_AT + 3)
        def _():
            whole_arrive()

        @pl.when((index >= RANKS_AT) & (index < RANKS_AT + (plan.tp - 1) * PARTS))
        def _():
            whole_to_rank((index - RANKS_AT) % (plan.tp - 1) + 1, (index - RANKS_AT) // (plan.tp - 1))

        @pl.when(index < layers)
        def _():
            make_layer(index, slot)

        @pl.when(index >= layers)
        def _():
            make_head(index, slot)

        send_own(slab_view(index), index, slot, chunk)

        @pl.when(index >= LAG)
        def _():
            forward(slab_view(index - LAG), index - LAG, chunk)

        @pl.when(index >= 2 * LAG)
        def _():
            forward_diagonal(slab_view(index - 2 * LAG), index - 2 * LAG, chunk)

        return 0

    lax.fori_loop(0, ring, step, 0)

    make_tail(ring % 2)
    send_own(slab_view(ring), ring, ring % 2, tail)
    make_extra()
    for index in range(ring - LAG, ring):
        forward(slab_view(index), index, chunk)
        if index == ring - LAG:
            whole_to_pair()
    forward(slab_view(ring), ring, tail)
    for index in range(ring - 2 * LAG, ring):
        forward_diagonal(slab_view(index), index, chunk)
        if index == ring - 2:
            sent = pl.ds(0, (plan.tp - 1) * rows)
            wait_for(packed, z_send.at[0])
            wait_for(zbuf.at[pl.ds(layers, last - layers), sent, pl.ds(0, chunk)], z_send.at[1])
            wait_for(zbuf.at[last, sent, pl.ds(0, plan.tail_window)], z_send.at[2])
            whole_finish()
            for n, own in enumerate((own_0, own_1)):
                wait_for(own.at[:, pl.ds(0, plan.cut)], share_recv.at[n])
                for parts in (8, 5):
                    gone = pl.ds(0, parts * (plan.down_rows + plan.out_rows))
                    wait_for(own.at[gone, pl.ds(0, plan.cut)], share_send.at[n])
            for index in range((ring - LAG) // COUNTED):
                finish(index, pl.ds(index * COUNTED, COUNTED), chunk)
    forward_diagonal(slab_view(ring), ring, tail)
    for index in range((ring - LAG) // COUNTED, plan.counts - 1):
        first = index * COUNTED
        finish(index, pl.ds(first, min(COUNTED, ring - first)), chunk)
    finish(plan.counts - 1, pl.ds(ring, 1), tail)


def gather(plan, *args):
    dma = pltpu.SemaphoreType.DMA
    groups = plan.layers // GROUP
    share_rows = plan.down_rows + plan.out_rows
    hbm = pl.BlockSpec(memory_space=pltpu.HBM)
    shapes = [(plan.dp, plan.ring + 1, plan.chunk, LANES), (plan.piece, plan.columns), (plan.piece, plan.columns)]
    shapes += [(plan.layers, plan.piece, plan.whole)] + [(plan.dp, share_rows, plan.cut)] * 2
    shapes += [(plan.tp, plan.layers, count, plan.whole) for count in (plan.down_rows, plan.out_rows)]
    return pl.pallas_call(
        functools.partial(gather_kernel, plan),
        out_shape=[jax.ShapeDtypeStruct(shape, jnp.bfloat16) for shape in shapes],
        in_specs=[hbm] * 8,
        out_specs=[hbm] * len(shapes),
        scratch_shapes=[
            pltpu.VMEM((plan.chunks, plan.tp * plan.rows, plan.layer_window), jnp.bfloat16),
            pltpu.VMEM((2, plan.chunk + 2 * LANES, LANES), jnp.bfloat16),
            dma((groups + plan.head_chunks,)), dma((3,)), dma((2,)),
            dma((SLOTS,)), dma((SLOTS,)), dma((SLOTS,)), dma((SLOTS,)), dma((plan.counts,)), dma((plan.counts,)),
            dma((2, plan.dp)), dma((2,)), dma((2,)),
            dma((8,)), dma((2,)), dma((2,)), dma((2,)), dma((2,)), dma((2,)),
            pltpu.VMEM((plan.layers, plan.down_rows, plan.whole), jnp.bfloat16),
            pltpu.VMEM((plan.layers, plan.out_rows, plan.whole), jnp.bfloat16),
            dma((4,)),
            pltpu.VMEM((plan.layers // GROUP, plan.tp - 1, GROUP, plan.rows, plan.layer_window), jnp.bfloat16),
            dma((plan.layers // GROUP,)),
        ],
        compiler_params=pltpu.CompilerParams(collective_id=0, has_side_effects=True),
        name="gather",
    )(*args)[:4]


def place_slabs(plan, slabs, first, count, shapes, store, held=()):
    hbm = pl.BlockSpec(memory_space=pltpu.HBM)
    depth = min(BUFFERS, count)
    ahead = depth // 2

    def body(slab, *refs):
        outs, (buffers, loads, stores) = refs[len(held):-3], refs[-3:]

        def each_size(chunk, act):
            if first + count > plan.ring:
                pl.when(chunk < plan.ring)(lambda: act(plan.chunk))
                pl.when(chunk == plan.ring)(lambda: act(plan.tail))
            else:
                act(plan.chunk)

        def load(i, rows):
            for owner in range(plan.dp):
                pltpu.make_async_copy(
                    slab.at[owner, first + i, pl.ds(0, rows), :],
                    buffers.at[i % depth, pl.ds(0, rows), pl.ds(owner * LANES, LANES)],
                    loads.at[i % depth],
                ).start()

        def wait(i, rows, sem):
            buffer = buffers.at[i % depth, pl.ds(0, rows), :]
            pltpu.make_async_copy(buffer, buffer, sem.at[i % depth]).wait()

        def write(i, rows):
            wait(i, rows, loads)
            for source, target in store(buffers.at[i % depth], first + i, rows, outs):
                pltpu.make_async_copy(source, target, stores.at[i % depth]).start()

        def step(i, _):
            @pl.when(i >= depth)
            def _():
                each_size(first + i - depth, lambda rows: wait(i - depth, rows, stores))

            @pl.when(i < count)
            def _():
                each_size(first + i, lambda rows: load(i, rows))

            @pl.when((i >= ahead) & (i < count + ahead))
            def _():
                each_size(first + i - ahead, lambda rows: write(i - ahead, rows))

            return 0

        lax.fori_loop(0, count + depth, step, 0)

    outs = [jax.ShapeDtypeStruct(shape, jnp.bfloat16) for shape in shapes]
    return pl.pallas_call(
        body,
        in_specs=[hbm] * (1 + len(held)),
        out_specs=[hbm] * len(outs),
        out_shape=outs,
        scratch_shapes=[
            pltpu.VMEM((depth, plan.chunk, plan.dp * LANES), jnp.bfloat16),
            pltpu.SemaphoreType.DMA((depth,)),
            pltpu.SemaphoreType.DMA((depth,)),
        ],
        input_output_aliases={1 + n: n for n in range(len(held))},
        cost_estimate=pl.CostEstimate(
            flops=10**7, bytes_accessed=4 * count * plan.chunk * plan.dp * LANES, transcendentals=0
        ),
        compiler_params=pltpu.CompilerParams(vmem_limit_bytes=VMEM),
    )(slabs, *held)


def place_layers(plan, slabs):
    narrow, wide, width = 3 * plan.part, 2 * plan.wide, plan.dp * LANES

    def store(buffer, chunk, rows, outs):
        return [
            (buffer.at[pl.ds(0, narrow), :], outs[0].at[chunk]),
            (buffer.at[pl.ds(narrow, wide), :], outs[1].at[chunk]),
        ]

    shapes = [(plan.layers, narrow, width), (plan.layers, wide, width)]
    return place_slabs(plan, slabs, 0, plan.layers, shapes, store)


def place_head(plan, slabs, first, count, *held):
    def store(buffer, chunk, rows, outs):
        at = pl.multiple_of((chunk - plan.layers) * plan.chunk, 16)
        return [(buffer.at[pl.ds(0, rows), :], outs[0].at[pl.ds(at, rows), :])]

    shapes = [(plan.vocab, plan.dp * LANES)]
    return place_slabs(plan, slabs, plan.layers + first, count, shapes, store, held)[0]


def place_rows(plan, arrays, spots, width, column, held):
    count = len(spots([array for array in arrays], 0))
    columns = arrays[0].shape[-1]
    outs = [
        jax.ShapeDtypeStruct((plan.layers, plan.downs, plan.columns), jnp.bfloat16),
        jax.ShapeDtypeStruct((plan.layers, plan.columns, plan.outs), jnp.bfloat16),
        jax.ShapeDtypeStruct((plan.vocab, plan.dp * LANES), jnp.bfloat16),
    ]
    with_head = columns > width
    kept = [n for n in range(3) if n in held]
    made = [n for n in range(3 if with_head else 2)]

    blocks = [(plan.downs, plan.outs), (0, plan.downs // 2), (plan.downs // 2, plan.downs // 2)]

    def body(*refs):
        targets = dict(zip(made, refs[len(arrays) + len(kept):-4], strict=True))
        buffers, turned, loads, stored = refs[-4:]
        moves = spots(refs[: len(arrays)], lax.axis_index("dp"))
        place = pl.ds(column, width)
        loading, storing = [], []
        for n, (source, _, _, _) in enumerate(moves):
            for b, (first, height) in enumerate(blocks):
                some = pl.ds(first, height)
                loading.append(pltpu.make_async_copy(source.at[some, :], buffers.at[n, some, :], loads.at[n, b]))
                loading[-1].start()

        def put(source, target):
            storing.append(pltpu.make_async_copy(source, target, stored.at[0]))
            storing[-1].start()

        for n, (_, layer, owner, part) in enumerate(moves):
            for b, (first, height) in enumerate(blocks):
                loading[n * len(blocks) + b].wait()
                some = pl.ds(first, height)
                if b:
                    put(buffers.at[n, some, pl.ds(0, width)], targets[0].at[layer, some, place])
                for j in range((columns - width) // LANES):
                    row = plan.extra_first + (part * WHOLE + j) * plan.piece + first
                    put(
                        buffers.at[n, some, pl.ds(width + j * LANES, LANES)],
                        targets[2].at[pl.ds(row, height), pl.ds(pl.multiple_of(owner * LANES, LANES), LANES)],
                    )
                if b:
                    continue
                for i in range(plan.outs // LANES):
                    for j in range(width // LANES):
                        turned[n, pl.ds(j * LANES, LANES), pl.ds(i * LANES, LANES)] = buffers[
                            n, pl.ds(plan.downs + i * LANES, LANES), pl.ds(j * LANES, LANES)
                        ].T
                put(turned.at[n], targets[1].at[layer, place, :])
        for store in storing:
            store.wait()

    hbm = pl.BlockSpec(memory_space=pltpu.HBM)
    dma = pltpu.SemaphoreType.DMA
    result = pl.pallas_call(
        body,
        out_shape=[outs[n] for n in made],
        in_specs=[hbm] * (len(arrays) + len(kept)),
        out_specs=[hbm] * len(made),
        scratch_shapes=[
            pltpu.VMEM((count, plan.piece, columns), jnp.bfloat16),
            pltpu.VMEM((count, width, plan.outs), jnp.bfloat16),
            dma((count, len(blocks))), dma((1,)),
        ],
        input_output_aliases={len(arrays) + i: n for i, n in enumerate(kept)},
        cost_estimate=pl.CostEstimate(flops=10**7, bytes_accessed=4 * count * plan.piece * columns, transcendentals=0),
        compiler_params=pltpu.CompilerParams(vmem_limit_bytes=VMEM),
    )(*arrays, *(held[n] for n in kept))
    return dict(zip(made, result, strict=True))


def place_whole(plan, whole):
    def spots(refs, dp):
        return [(refs[0].at[layer], layer, 0, 0) for layer in range(plan.layers)]

    return place_rows(plan, [whole], spots, plan.whole, 0, {})


def place_shares(plan, shares, held):
    which = [(owner, part) for owner, arrays in shares.items() for part in arrays]
    arrays = [shares[owner][part] for owner, part in which]

    def spots(refs, dp):
        core, x, y = dp % 2, (dp // 2) % 2, dp // 4
        found = []
        for ref, ((flip_x, flip_y, flip_core), part) in zip(refs, which, strict=True):
            owner = (y + flip_y * (1 - 2 * y)) * 4 + (x + flip_x * (1 - 2 * x)) * 2 + core + flip_core * (1 - 2 * core)
            found.append((ref, owner * plan.share + part, owner, part))
        return found

    return place_rows(plan, arrays, spots, plan.cut, plan.whole, held)


def solution(mesh):
    train_stack = P(None, ("dp", "tp"), None)
    train_head = P(("dp", "tp"), None)
    fused_stack = P(None, "tp", None)
    last_stack = P(None, None, "tp")
    head_rows = P("tp", None)

    def local_sync(w_query, w_key, w_value, w_out, w_gate, w_up, w_down, w_head):
        plan = Plan(mesh.shape["tp"], mesh.shape["dp"], w_query, w_gate, w_out, w_down, w_head)
        slabs, own_0, own_1, whole = gather(plan, w_query, w_key, w_value, w_out, w_gate, w_up, w_down, w_head)

        def swap(bit, array):
            return lax.ppermute(array, "dp", [(i, i ^ bit) for i in range(plan.dp)])

        pair, along_x, along_y = (functools.partial(swap, bit) for bit in (1, 2, 4))
        hold = lax.optimization_barrier

        x_1, y_0 = along_x(own_1), along_y(own_0)
        x_0, y_1 = along_x(own_0), along_y(own_1)
        pair_own = [pair(own_0), pair(own_1)]
        qkv_block, gate_up_block = place_layers(plan, slabs)
        x_1, y_0, qkv_block, slabs = hold((x_1, y_0, qkv_block, slabs))
        diagonal_0 = along_x(y_0)
        diagonal_1 = along_y(x_1)
        pair_x_1, pair_y_0 = pair(x_1), pair(y_0)
        head_chunks = plan.ring + 1 - plan.layers
        early = head_chunks // 4
        head_block = place_head(plan, slabs, early, head_chunks - early)
        x_0, y_1, head_block, slabs, whole = hold((x_0, y_1, head_block, slabs, whole))
        pair_x_0, pair_y_1 = pair(x_0), pair(y_1)
        placed = place_whole(plan, whole)
        slabs, *placed = hold((slabs, placed[0], placed[1]))
        head_block = place_head(plan, slabs, 0, early, head_block)
        own_0, own_1, head_block = hold((own_0, own_1, head_block))
        near = {
            (0, 0, 0): {0: own_0, 1: own_1}, (0, 0, 1): dict(enumerate(pair_own)),
            (1, 0, 0): {0: x_0, 1: x_1}, (1, 0, 1): {0: pair_x_0, 1: pair_x_1},
            (0, 1, 0): {0: y_0, 1: y_1}, (0, 1, 1): {0: pair_y_0, 1: pair_y_1},
        }
        placed = place_shares(plan, near, {0: placed[0], 1: placed[1], 2: head_block})
        diagonal_0, head_block = hold((diagonal_0, placed[2]))
        pair_diagonal_0 = pair(diagonal_0)
        diagonal_1, down_block = hold((diagonal_1, placed[0]))
        pair_diagonal_1 = pair(diagonal_1)
        placed = {0: down_block, 1: placed[1], 2: head_block}
        placed = place_shares(plan, {(1, 1, 0): {0: diagonal_0, 1: diagonal_1}}, placed)
        placed = place_shares(plan, {(1, 1, 1): {0: pair_diagonal_0}}, placed)
        placed = place_shares(plan, {(1, 1, 1): {1: pair_diagonal_1}}, placed)
        down_block, o_block, head_block = placed[0], placed[1], placed[2]
        return (
            qkv_block,
            o_block,
            gate_up_block,
            jnp.swapaxes(down_block, 1, 2),
            head_block,
        )

    return jax.shard_map(
        local_sync,
        mesh=mesh,
        in_specs=(train_stack,) * 7 + (train_head,),
        out_specs=(fused_stack, last_stack, fused_stack, last_stack, head_rows),
        check_vma=False,
    )
```

profile of v0, /device:TPU:0, one launch (start us, length us, event | category | flops | bytes accessed | tf_op | source)
XLA Modules:
  0.0 782.2 jit_solution(5188494326417041460)
XLA Ops:
  0.6 635.4 %gather.1 = (bf16[8,31,2176,128]{3,2,1,0:T(8,128)(2,1)}, bf16[960,1024]{1,0:T(8,128)(2,1)}, bf16[960,1024]{1,0:T(8,128)(2,1)}, bf16[16,960,384]{2,1,0:T(8,128)(2...) custom-call(bf16[16,32,1024]{2,1,0:T(8,128)(2,1)} %q.1, ...), custom_call_target="tpu_custom_call" | custom-call | tf_op jit(solution)/shard_map/gather/pallas_call | solution.py:502
  636.0 1.6 collective-permute-start
  637.6 0.5 collective-permute-start.1
  638.1 1.5 collective-permute-start.3
  639.6 0.5 collective-permute-start.4
  640.2 45.5 %shard_map.119 = (bf16[16,768,1024]{2,1,0:T(8,128)(2,1)}, bf16[16,1408,1024]{2,1,0:T(8,128)(2,1)}) custom-call(bf16[8,31,2176,128]{3,2,1,0:T(8,128)(2,1)} %get-tuple-element.56.slab), custom_call_target="tpu_custom_call" | custom-call | flops 10000000 | bytes 142606336 | tf_op jit(solution)/shard_map/pallas_call | solution.py:575
  685.6 0.6 collective-permute-start.6
  686.2 34.0 %shard_map.120.refs_0_ = bf16[37984,1024]{1,0:T(8,128)(2,1)} custom-call(bf16[8,31,2176,128]{3,2,1,0:T(8,128)(2,1)} %get-tuple-element.56.slab), custom_call_target="tpu_custom_call" | custom-call | flops 10000000 | bytes 106954752 | tf_op jit(solution)/shard_map/pallas_call | solution.py:575
  720.2 3.2 collective-permute-done.3.refs_4_
  723.4 1.2 collective-permute-done.4.refs_9_
  724.6 0.5 collective-permute-start.7
  725.1 0.0 collective-permute-start.8
  725.1 0.5 collective-permute-start.9
  725.7 0.5 collective-permute-start.12
  726.2 2.8 collective-permute-done.10.refs_11_
  728.9 0.5 collective-permute-start.2
  729.5 8.9 %shard_map.121 = (bf16[16,704,1024]{2,1,0:T(8,128)(2,1)}, bf16[16,1024,256]{2,1,0:T(8,128)(2,1)}) custom-call(bf16[16,960,384]{2,1,0:T(8,128)(2,1)} %get-tuple-element.53.refs_0_), custom_call_target="tpu_custom_call" | custom-call | flops 10000000 | bytes 23592960 | tf_op jit(solution)/shard_map/pallas_call | solution.py:670
  738.4 10.4 %shard_map.122.refs_14_ = bf16[37984,1024]{1,0:T(8,128)(2,1)} custom-call(bf16[8,31,2176,128]{3,2,1,0:T(8,128)(2,1)} %get-tuple-element.56.slab, bf16[37984,1024]{1,0:T(8,128)(2,1)} %shard_map.120.refs_0_), custom_call_target="tpu_custom_call", output_to_operand_aliasing={{}: (1, {})} | custom-call | flops 10000000 | bytes 26738688 | tf_op jit(solution)/shard_map/pallas_call | solution.py:575
  748.8 15.9 %shard_map.123 = (bf16[16,704,1024]{2,1,0:T(8,128)(2,1)}, bf16[16,1024,256]{2,1,0:T(8,128)(2,1)}, bf16[37984,1024]{1,0:T(8,128)(2,1)}) custom-call(bf16[960,1024]{1,0:T(8,128)(2,1)} %get-tuple-element.58.refs_0_, bf16[960,1024]{1,0:T(8,128)(2,1)} %get-tuple-element.59.refs_1_, ...), custom_call_target="tpu_custom_call", output_to_operand_aliasing={{0}: (12, {}), {1}: (13, {}), {2}: (14, {})} | custom-call | flops 10000000 | bytes 47185920 | tf_op jit(solution)/shard_map/pallas_call | solution.py:670
  764.8 6.0 collective-permute-done.12.refs_0_
  770.8 3.3 collective-permute-done.2.refs_1_
  774.1 3.2 shard_map.124
  777.3 2.4 shard_map.125
  779.8 2.4 shard_map.126
  (13 shorter events, 0.0 us)
Async XLA Ops:
  636.0 49.6 %collective-permute-start = (bf16[960,1024]{1,0:T(8,128)(2,1)}, bf16[960,1024]{1,0:T(8,128)(2,1)}, u32[]{:S(2)}, u32[]{:S(2)}) collective-permute-start(bf16[960,1024]{1,0:T(8,128)(2,1)} %get-tuple-element.59.refs_1_), channel_id=1, source_target_pairs={{0,2},{1,3},{2,0},{3,1},{4,6},{5,7},{6,4},{7,5},{8,10},{9,11},{10,... | collective-permute-start | bytes 5898248 | tf_op jit(solution)/shard_map/ppermute | solution.py:721
  637.6 48.6 %collective-permute-start.1 = (bf16[960,1024]{1,0:T(8,128)(2,1)}, bf16[960,1024]{1,0:T(8,128)(2,1)}, u32[]{:S(2)}, u32[]{:S(2)}) collective-permute-start(bf16[960,1024]{1,0:T(8,128)(2,1)} %get-tuple-element.58.refs_0_), channel_id=1, source_target_pairs={{0,4},{1,5},{2,6},{3,7},{4,0},{5,1},{6,2},{7,3},{8,12},{9,13},{10,... | collective-permute-start | bytes 5898248 | tf_op jit(solution)/shard_map/ppermute | solution.py:721
  638.1 85.3 %collective-permute-start.3 = (bf16[960,1024]{1,0:T(8,128)(2,1)}, bf16[960,1024]{1,0:T(8,128)(2,1)}, u32[]{:S(2)}, u32[]{:S(2)}) collective-permute-start(bf16[960,1024]{1,0:T(8,128)(2,1)} %get-tuple-element.58.refs_0_), channel_id=1, source_target_pairs={{0,2},{1,3},{2,0},{3,1},{4,6},{5,7},{6,4},{7,5},{8,10},{9,11},{10,... | collective-permute-start | bytes 5898248 | tf_op jit(solution)/shard_map/ppermute | solution.py:721
  639.6 85.0 %collective-permute-start.4 = (bf16[960,1024]{1,0:T(8,128)(2,1)}, bf16[960,1024]{1,0:T(8,128)(2,1)}, u32[]{:S(2)}, u32[]{:S(2)}) collective-permute-start(bf16[960,1024]{1,0:T(8,128)(2,1)} %get-tuple-element.59.refs_1_), channel_id=1, source_target_pairs={{0,4},{1,5},{2,6},{3,7},{4,0},{5,1},{6,2},{7,3},{8,12},{9,13},{10,... | collective-permute-start | bytes 5898248 | tf_op jit(solution)/shard_map/ppermute | solution.py:721
  640.2 85.0 %collective-permute-start.5 = (bf16[960,1024]{1,0:T(8,128)(2,1)}, bf16[960,1024]{1,0:T(8,128)(2,1)}, u32[]{:S(2)}, u32[]{:S(2)}) collective-permute-start(bf16[960,1024]{1,0:T(8,128)(2,1)} %get-tuple-element.58.refs_0_), channel_id=1, source_target_pairs={{0,1},{1,0},{2,3},{3,2},{4,5},{5,4},{6,7},{7,6},{8,9},{9,8},{10,11... | collective-permute-start | bytes 5898248 | tf_op jit(solution)/shard_map/ppermute | solution.py:721
  685.6 40.0 %collective-permute-start.6 = (bf16[960,1024]{1,0:T(8,128)(2,1)}, bf16[960,1024]{1,0:T(8,128)(2,1)}, u32[]{:S(2)}, u32[]{:S(2)}) collective-permute-start(bf16[960,1024]{1,0:T(8,128)(2,1)} %get-tuple-element.59.refs_1_), channel_id=1, source_target_pairs={{0,1},{1,0},{2,3},{3,2},{4,5},{5,4},{6,7},{7,6},{8,9},{9,8},{10,11... | collective-permute-start | bytes 5898248 | tf_op jit(solution)/shard_map/ppermute | solution.py:721
  724.6 4.3 collective-permute-start.10
  724.6 24.2 %collective-permute-start.7 = (bf16[960,1024]{1,0:T(8,128)(2,1)}, bf16[960,1024]{1,0:T(8,128)(2,1)}, u32[]{:S(2)}, u32[]{:S(2)}) collective-permute-start(bf16[960,1024]{1,0:T(8,128)(2,1)} %collective-permute-done.3.refs_4_), channel_id=1, source_target_pairs={{0,1},{1,0},{2,3},{3,2},{4,5},{5,4},{6,7},{7,6},{8,9},{9,8},{10,11... | collective-permute-start | bytes 5898248 | tf_op jit(solution)/shard_map/ppermute | solution.py:721
  725.1 23.7 %collective-permute-start.8 = (bf16[960,1024]{1,0:T(8,128)(2,1)}, bf16[960,1024]{1,0:T(8,128)(2,1)}, u32[]{:S(2)}, u32[]{:S(2)}) collective-permute-start(bf16[960,1024]{1,0:T(8,128)(2,1)} %collective-permute-done.refs_5_), channel_id=1, source_target_pairs={{0,1},{1,0},{2,3},{3,2},{4,5},{5,4},{6,7},{7,6},{8,9},{9,8},{10,11... | collective-permute-start | bytes 5898248 | tf_op jit(solution)/shard_map/ppermute | solution.py:721
  725.1 23.7 %collective-permute-start.9 = (bf16[960,1024]{1,0:T(8,128)(2,1)}, bf16[960,1024]{1,0:T(8,128)(2,1)}, u32[]{:S(2)}, u32[]{:S(2)}) collective-permute-start(bf16[960,1024]{1,0:T(8,128)(2,1)} %collective-permute-done.1.refs_8_), channel_id=1, source_target_pairs={{0,1},{1,0},{2,3},{3,2},{4,5},{5,4},{6,7},{7,6},{8,9},{9,8},{10,11... | collective-permute-start | bytes 5898248 | tf_op jit(solution)/shard_map/ppermute | solution.py:721
  725.7 45.1 %collective-permute-start.12 = (bf16[960,1024]{1,0:T(8,128)(2,1)}, bf16[960,1024]{1,0:T(8,128)(2,1)}, u32[]{:S(2)}, u32[]{:S(2)}) collective-permute-start(bf16[960,1024]{1,0:T(8,128)(2,1)} %collective-permute-done.1.refs_8_), channel_id=1, source_target_pairs={{0,2},{1,3},{2,0},{3,1},{4,6},{5,7},{6,4},{7,5},{8,10},{9,11},{10,... | collective-permute-start | bytes 5898248 | tf_op jit(solution)/shard_map/ppermute | solution.py:721
  728.9 45.2 %collective-permute-start.2 = (bf16[960,1024]{1,0:T(8,128)(2,1)}, bf16[960,1024]{1,0:T(8,128)(2,1)}, u32[]{:S(2)}, u32[]{:S(2)}) collective-permute-start(bf16[960,1024]{1,0:T(8,128)(2,1)} %collective-permute-done.refs_5_), channel_id=1, source_target_pairs={{0,4},{1,5},{2,6},{3,7},{4,0},{5,1},{6,2},{7,3},{8,12},{9,13},{10,... | collective-permute-start | bytes 5898248 | tf_op jit(solution)/shard_map/ppermute | solution.py:721
  770.8 6.6 collective-permute-start.13
  774.1 5.6 collective-permute-start.11
where the time goes:
time: 782 us
  Pallas kernels  758 us (97%)
  waiting for transfers between devices  16.5 us (2%)
    pallas_call x1, Pallas kernels, gather(): pl.pallas_call(functools.partial(gather_kernel, plan), out_shape=[jax.Sha...  635 us
    pallas_call x3, Pallas kernels, place_slabs(): pl.pallas_call(body, in_specs=[hbm] * (1 + len(held)), out_specs=[hbm] *...  89.8 us
    pallas_call x5, Pallas kernels, place_rows(): pl.pallas_call(body, out_shape=[outs[n] for n in made], in_specs=[hbm] *...  32.8 us
    ppermute x14, waiting for transfers between devices, swap(): return lax.ppermute(array, 'dp', [(i, i ^ bit) for i in range(plan.dp)])  16.5 us
  transfers between devices with their start and end apart: 14, of which 5 were waited for; matrix products, arithmetic and copies ran while one was open for 0% of the time, Pallas kernels for 15%

commit v1 on v0

--- a/solution.py
+++ b/solution.py
@@ -15,7 +15,7 @@
 BUFFERS = 6
 LAG = 1
 SHARE_AT = 20
-SLOTS = 8
+SLOTS = 4
 COUNTED = 4
 WHOLE = 3
 WHOLE_AT = 2
@@ -61,7 +61,7 @@
         return base - (rank // (self.tp - 1)) * (self.vocab * (self.tp - 1) // LANES + self.window_tiles - self.head_tiles)
 
 
-def gather_kernel(plan, q, k, v, o, g, u, d, h, slabs, own_0, own_1, whole, stop_0, stop_1, land_d, land_o, zbuf, tbuf,
+def gather_kernel(plan, q, k, v, o, g, u, d, h, slabs, own_0, own_1, whole, stop, land_d, land_o, zbuf, tbuf,
                   z_recv, z_send, local, x_recv, y_recv, a_recv, b_recv, pair_recv, send, stop_recv, share_recv,
                   share_send, land_recv, land_send, whole_recv, whole_send, whole_pair_recv, whole_pair_send,
                   keep_d, keep_o, keep_sem, packed, pack_sem):
@@ -259,10 +259,10 @@
         stop_downs, stop_outs = pl.ds(0, plan.down_rows), pl.ds(plan.down_rows, plan.out_rows)
         cut, home = pl.ds(plan.whole, plan.cut), pl.ds(0, plan.cut)
         found = []
-        for n, (stop, own) in enumerate(((stop_0, own_0), (stop_1, own_1))):
+        for n, own in enumerate((own_0, own_1)):
             layer = to * 2 + n
-            found.append((d.at[layer, :, cut], stop.at[source_dp, stop_downs, :], own.at[downs, home], n))
-            found.append((o.at[layer, :, cut], stop.at[source_dp, stop_outs, :], own.at[outs, home], n))
+            found.append((d.at[layer, :, cut], stop.at[source_dp, n, stop_downs, :], own.at[downs, home], n))
+            found.append((o.at[layer, :, cut], stop.at[source_dp, n, stop_outs, :], own.at[outs, home], n))
         return found
 
     my_rank = dp // 2
@@ -280,8 +280,8 @@
 
             @pl.when(jnp.logical_not(stays))
             def _(to=to):
-                for part, stop, _, n in pieces(dp, to, my_place):
-                    remote(part, stop, share_send.at[n], stop_recv.at[n, dp], dp=to)
+                for part, waiting, _, n in pieces(dp, to, my_place):
+                    remote(part, waiting, share_send.at[n], stop_recv.at[dp], dp=to)
 
         @pl.when(stays)
         def _():
@@ -298,10 +298,9 @@
 
         @pl.when((rank != z) & (source_dp != dp))
         def _():
-            for n, stop in enumerate((stop_0, stop_1)):
-                wait_for(stop.at[source_dp], stop_recv.at[n, source_dp])
-            for _, stop, final, n in pieces(source_dp, dp, place):
-                remote(stop, final, share_send.at[n], share_recv.at[n], tp=rank)
+            wait_for(stop.at[source_dp], stop_recv.at[source_dp])
+            for _, waiting, final, n in pieces(source_dp, dp, place):
+                remote(waiting, final, share_send.at[n], share_recv.at[n], tp=rank)
 
 
     whole_columns = pl.ds(0, plan.whole)
@@ -497,7 +496,7 @@
     share_rows = plan.down_rows + plan.out_rows
     hbm = pl.BlockSpec(memory_space=pltpu.HBM)
     shapes = [(plan.dp, plan.ring + 1, plan.chunk, LANES), (plan.piece, plan.columns), (plan.piece, plan.columns)]
-    shapes += [(plan.layers, plan.piece, plan.whole)] + [(plan.dp, share_rows, plan.cut)] * 2
+    shapes += [(plan.layers, plan.piece, plan.whole), (plan.dp, plan.share, share_rows, plan.cut)]
     shapes += [(plan.tp, plan.layers, count, plan.whole) for count in (plan.down_rows, plan.out_rows)]
     return pl.pallas_call(
         functools.partial(gather_kernel, plan),
@@ -509,7 +508,7 @@
             pltpu.VMEM((2, plan.chunk + 2 * LANES, LANES), jnp.bfloat16),
             dma((groups + plan.head_chunks,)), dma((3,)), dma((2,)),
             dma((SLOTS,)), dma((SLOTS,)), dma((SLOTS,)), dma((SLOTS,)), dma((plan.counts,)), dma((plan.counts,)),
-            dma((2, plan.dp)), dma((2,)), dma((2,)),
+            dma((plan.dp,)), dma((2,)), dma((2,)),
             dma((8,)), dma((2,)), dma((2,)), dma((2,)), dma((2,)), dma((2,)),
             pltpu.VMEM((plan.layers, plan.down_rows, plan.whole), jnp.bfloat16),
             pltpu.VMEM((plan.layers, plan.out_rows, plan.whole), jnp.bfloat16),

time: 782 us -> 782 us (level)
  no operation moved by 1% of the time
where the time goes in v1:
time: 782 us
  Pallas kernels  758 us (97%)
  waiting for transfers between devices  16.5 us (2%)
    pallas_call x1, Pallas kernels, gather(): pl.pallas_call(functools.partial(gather_kernel, plan), out_shape=[jax.Sha...  635 us
    pallas_call x3, Pallas kernels, place_slabs(): pl.pallas_call(body, in_specs=[hbm] * (1 + len(held)), out_specs=[hbm] *...  89.8 us
    pallas_call x5, Pallas kernels, place_rows(): pl.pallas_call(body, out_shape=[outs[n] for n in made], in_specs=[hbm] *...  32.8 us
    ppermute x14, waiting for transfers between devices, swap(): return lax.ppermute(array, 'dp', [(i, i ^ bit) for i in range(plan.dp)])  16.5 us
  transfers between devices with their start and end apart: 14, of which 5 were waited for; matrix products, arithmetic and copies ran while one was open for 0% of the time, Pallas kernels for 15%

profile of v1, /device:TPU:0, one launch (start us, length us, event | category | flops | bytes accessed | tf_op | source)
XLA Modules:
  0.0 782.0 jit_solution(12979690936429399144)
XLA Ops:
  0.6 635.2 %gather.1 = (bf16[8,31,2176,128]{3,2,1,0:T(8,128)(2,1)}, bf16[960,1024]{1,0:T(8,128)(2,1)}, bf16[960,1024]{1,0:T(8,128)(2,1)}, bf16[16,960,384]{2,1,0:T(8,128)(2...) custom-call(bf16[16,32,1024]{2,1,0:T(8,128)(2,1)} %q.1, ...), custom_call_target="tpu_custom_call" | custom-call | tf_op jit(solution)/shard_map/gather/pallas_call | solution.py:501
  635.8 1.6 collective-permute-start
  637.4 0.5 collective-permute-start.1
  637.9 1.5 collective-permute-start.3
  639.4 0.5 collective-permute-start.4
  639.9 45.5 %shard_map.119 = (bf16[16,768,1024]{2,1,0:T(8,128)(2,1)}, bf16[16,1408,1024]{2,1,0:T(8,128)(2,1)}) custom-call(bf16[8,31,2176,128]{3,2,1,0:T(8,128)(2,1)} %get-tuple-element.56.slab), custom_call_target="tpu_custom_call" | custom-call | flops 10000000 | bytes 142606336 | tf_op jit(solution)/shard_map/pallas_call | solution.py:574
  685.4 0.6 collective-permute-start.6
  686.0 34.0 %shard_map.120.refs_0_ = bf16[37984,1024]{1,0:T(8,128)(2,1)} custom-call(bf16[8,31,2176,128]{3,2,1,0:T(8,128)(2,1)} %get-tuple-element.56.slab), custom_call_target="tpu_custom_call" | custom-call | flops 10000000 | bytes 106954752 | tf_op jit(solution)/shard_map/pallas_call | solution.py:574
  720.0 3.2 collective-permute-done.3.refs_4_
  723.2 1.2 collective-permute-done.4.refs_9_
  724.4 0.5 collective-permute-start.7
  724.9 0.0 collective-permute-start.8
  724.9 0.5 collective-permute-start.9
  725.4 0.5 collective-permute-start.12
  726.0 2.8 collective-permute-done.10.refs_11_
  728.7 0.5 collective-permute-start.2
  729.3 8.9 %shard_map.121 = (bf16[16,704,1024]{2,1,0:T(8,128)(2,1)}, bf16[16,1024,256]{2,1,0:T(8,128)(2,1)}) custom-call(bf16[16,960,384]{2,1,0:T(8,128)(2,1)} %get-tuple-element.53.refs_0_), custom_call_target="tpu_custom_call" | custom-call | flops 10000000 | bytes 23592960 | tf_op jit(solution)/shard_map/pallas_call | solution.py:669
  738.2 10.4 %shard_map.122.refs_14_ = bf16[37984,1024]{1,0:T(8,128)(2,1)} custom-call(bf16[8,31,2176,128]{3,2,1,0:T(8,128)(2,1)} %get-tuple-element.56.slab, bf16[37984,1024]{1,0:T(8,128)(2,1)} %shard_map.120.refs_0_), custom_call_target="tpu_custom_call", output_to_operand_aliasing={{}: (1, {})} | custom-call | flops 10000000 | bytes 26738688 | tf_op jit(solution)/shard_map/pallas_call | solution.py:574
  748.6 15.9 %shard_map.123 = (bf16[16,704,1024]{2,1,0:T(8,128)(2,1)}, bf16[16,1024,256]{2,1,0:T(8,128)(2,1)}, bf16[37984,1024]{1,0:T(8,128)(2,1)}) custom-call(bf16[960,1024]{1,0:T(8,128)(2,1)} %get-tuple-element.58.refs_0_, bf16[960,1024]{1,0:T(8,128)(2,1)} %get-tuple-element.59.refs_1_, ...), custom_call_target="tpu_custom_call", output_to_operand_aliasing={{0}: (12, {}), {1}: (13, {}), {2}: (14, {})} | custom-call | flops 10000000 | bytes 47185920 | tf_op jit(solution)/shard_map/pallas_call | solution.py:669
  764.6 6.0 collective-permute-done.12.refs_0_
  770.6 3.3 collective-permute-done.2.refs_1_
  773.9 3.2 shard_map.124
  777.1 2.4 shard_map.125
  779.5 2.4 shard_map.126
  (13 shorter events, 0.0 us)
Async XLA Ops:
  635.8 49.6 %collective-permute-start = (bf16[960,1024]{1,0:T(8,128)(2,1)}, bf16[960,1024]{1,0:T(8,128)(2,1)}, u32[]{:S(2)}, u32[]{:S(2)}) collective-permute-start(bf16[960,1024]{1,0:T(8,128)(2,1)} %get-tuple-element.59.refs_1_), channel_id=1, source_target_pairs={{0,2},{1,3},{2,0},{3,1},{4,6},{5,7},{6,4},{7,5},{8,10},{9,11},{10,... | collective-permute-start | bytes 5898248 | tf_op jit(solution)/shard_map/ppermute | solution.py:720
  637.4 48.6 %collective-permute-start.1 = (bf16[960,1024]{1,0:T(8,128)(2,1)}, bf16[960,1024]{1,0:T(8,128)(2,1)}, u32[]{:S(2)}, u32[]{:S(2)}) collective-permute-start(bf16[960,1024]{1,0:T(8,128)(2,1)} %get-tuple-element.58.refs_0_), channel_id=1, source_target_pairs={{0,4},{1,5},{2,6},{3,7},{4,0},{5,1},{6,2},{7,3},{8,12},{9,13},{10,... | collective-permute-start | bytes 5898248 | tf_op jit(solution)/shard_map/ppermute | solution.py:720
  637.9 85.3 %collective-permute-start.3 = (bf16[960,1024]{1,0:T(8,128)(2,1)}, bf16[960,1024]{1,0:T(8,128)(2,1)}, u32[]{:S(2)}, u32[]{:S(2)}) collective-permute-start(bf16[960,1024]{1,0:T(8,128)(2,1)} %get-tuple-element.58.refs_0_), channel_id=1, source_target_pairs={{0,2},{1,3},{2,0},{3,1},{4,6},{5,7},{6,4},{7,5},{8,10},{9,11},{10,... | collective-permute-start | bytes 5898248 | tf_op jit(solution)/shard_map/ppermute | solution.py:720
  639.4 85.0 %collective-permute-start.4 = (bf16[960,1024]{1,0:T(8,128)(2,1)}, bf16[960,1024]{1,0:T(8,128)(2,1)}, u32[]{:S(2)}, u32[]{:S(2)}) collective-permute-start(bf16[960,1024]{1,0:T(8,128)(2,1)} %get-tuple-element.59.refs_1_), channel_id=1, source_target_pairs={{0,4},{1,5},{2,6},{3,7},{4,0},{5,1},{6,2},{7,3},{8,12},{9,13},{10,... | collective-permute-start | bytes 5898248 | tf_op jit(solution)/shard_map/ppermute | solution.py:720
  639.9 85.0 %collective-permute-start.5 = (bf16[960,1024]{1,0:T(8,128)(2,1)}, bf16[960,1024]{1,0:T(8,128)(2,1)}, u32[]{:S(2)}, u32[]{:S(2)}) collective-permute-start(bf16[960,1024]{1,0:T(8,128)(2,1)} %get-tuple-element.58.refs_0_), channel_id=1, source_target_pairs={{0,1},{1,0},{2,3},{3,2},{4,5},{5,4},{6,7},{7,6},{8,9},{9,8},{10,11... | collective-permute-start | bytes 5898248 | tf_op jit(solution)/shard_map/ppermute | solution.py:720
  685.4 40.0 %collective-permute-start.6 = (bf16[960,1024]{1,0:T(8,128)(2,1)}, bf16[960,1024]{1,0:T(8,128)(2,1)}, u32[]{:S(2)}, u32[]{:S(2)}) collective-permute-start(bf16[960,1024]{1,0:T(8,128)(2,1)} %get-tuple-element.59.refs_1_), channel_id=1, source_target_pairs={{0,1},{1,0},{2,3},{3,2},{4,5},{5,4},{6,7},{7,6},{8,9},{9,8},{10,11... | collective-permute-start | bytes 5898248 | tf_op jit(solution)/shard_map/ppermute | solution.py:720
  724.4 4.3 collective-permute-start.10
  724.4 24.2 %collective-permute-start.7 = (bf16[960,1024]{1,0:T(8,128)(2,1)}, bf16[960,1024]{1,0:T(8,128)(2,1)}, u32[]{:S(2)}, u32[]{:S(2)}) collective-permute-start(bf16[960,1024]{1,0:T(8,128)(2,1)} %collective-permute-done.3.refs_4_), channel_id=1, source_target_pairs={{0,1},{1,0},{2,3},{3,2},{4,5},{5,4},{6,7},{7,6},{8,9},{9,8},{10,11... | collective-permute-start | bytes 5898248 | tf_op jit(solution)/shard_map/ppermute | solution.py:720
  724.9 23.7 %collective-permute-start.8 = (bf16[960,1024]{1,0:T(8,128)(2,1)}, bf16[960,1024]{1,0:T(8,128)(2,1)}, u32[]{:S(2)}, u32[]{:S(2)}) collective-permute-start(bf16[960,1024]{1,0:T(8,128)(2,1)} %collective-permute-done.refs_5_), channel_id=1, source_target_pairs={{0,1},{1,0},{2,3},{3,2},{4,5},{5,4},{6,7},{7,6},{8,9},{9,8},{10,11... | collective-permute-start | bytes 5898248 | tf_op jit(solution)/shard_map/ppermute | solution.py:720
  724.9 23.7 %collective-permute-start.9 = (bf16[960,1024]{1,0:T(8,128)(2,1)}, bf16[960,1024]{1,0:T(8,128)(2,1)}, u32[]{:S(2)}, u32[]{:S(2)}) collective-permute-start(bf16[960,1024]{1,0:T(8,128)(2,1)} %collective-permute-done.1.refs_8_), channel_id=1, source_target_pairs={{0,1},{1,0},{2,3},{3,2},{4,5},{5,4},{6,7},{7,6},{8,9},{9,8},{10,11... | collective-permute-start | bytes 5898248 | tf_op jit(solution)/shard_map/ppermute | solution.py:720
  725.4 45.1 %collective-permute-start.12 = (bf16[960,1024]{1,0:T(8,128)(2,1)}, bf16[960,1024]{1,0:T(8,128)(2,1)}, u32[]{:S(2)}, u32[]{:S(2)}) collective-permute-start(bf16[960,1024]{1,0:T(8,128)(2,1)} %collective-permute-done.1.refs_8_), channel_id=1, source_target_pairs={{0,2},{1,3},{2,0},{3,1},{4,6},{5,7},{6,4},{7,5},{8,10},{9,11},{10,... | collective-permute-start | bytes 5898248 | tf_op jit(solution)/shard_map/ppermute | solution.py:720
  728.7 45.2 %collective-permute-start.2 = (bf16[960,1024]{1,0:T(8,128)(2,1)}, bf16[960,1024]{1,0:T(8,128)(2,1)}, u32[]{:S(2)}, u32[]{:S(2)}) collective-permute-start(bf16[960,1024]{1,0:T(8,128)(2,1)} %collective-permute-done.refs_5_), channel_id=1, source_target_pairs={{0,4},{1,5},{2,6},{3,7},{4,0},{5,1},{6,2},{7,3},{8,12},{9,13},{10,... | collective-permute-start | bytes 5898248 | tf_op jit(solution)/shard_map/ppermute | solution.py:720
  770.6 6.6 collective-permute-start.13
  773.9 5.6 collective-permute-start.11

commit v2 on v1

--- a/solution.py
+++ b/solution.py
@@ -15,7 +15,8 @@
 BUFFERS = 6
 LAG = 1
 SHARE_AT = 20
-SLOTS = 4
+LAST = 256
+SLOTS = 5
 COUNTED = 4
 WHOLE = 3
 WHOLE_AT = 2
@@ -221,11 +222,14 @@
         remote(part, part, send.at[counted(index)], pair_recv.at[counted(index)], dp=pair)
 
     def counted(index):
-        return plan.counts - 1 if index is ring else index // COUNTED
+        return plan.counts - 1 if isinstance(index, int) and index >= ring else index // COUNTED
 
     def send_own(view, index, slot, count):
         own = view(dp, 0, count)
         wait_for(own, local.at[slot])
+        push_own(own, index)
+
+    def push_own(own, index):
         push(own, index, x_recv, x_peer)
         push(own, index, y_recv, y_peer)
         push_pair(own, index)
@@ -460,14 +464,21 @@
 
     lax.fori_loop(0, ring, step, 0)
 
+    def part_view(start):
+        return lambda owner, first, count: slabs.at[owner, ring, pl.ds(start + first, count), :]
+
+    tail_parts = [(part_view(0), ring, tail - LAST), (part_view(tail - LAST), ring + 1, LAST)]
     make_tail(ring % 2)
-    send_own(slab_view(ring), ring, ring % 2, tail)
+    wait_for(slabs.at[dp, ring, pl.ds(0, tail), :], local.at[ring % 2])
+    for view, index, count in tail_parts:
+        push_own(view(dp, 0, count), index)
     make_extra()
     for index in range(ring - LAG, ring):
         forward(slab_view(index), index, chunk)
         if index == ring - LAG:
             whole_to_pair()
-    forward(slab_view(ring), ring, tail)
+    for part in tail_parts:
+        forward(*part)
     for index in range(ring - 2 * LAG, ring):
         forward_diagonal(slab_view(index), index, chunk)
         if index == ring - 2:
@@ -483,7 +494,8 @@
                     wait_for(own.at[gone, pl.ds(0, plan.cut)], share_send.at[n])
             for index in range((ring - LAG) // COUNTED):
                 finish(index, pl.ds(index * COUNTED, COUNTED), chunk)
-    forward_diagonal(slab_view(ring), ring, tail)
+    for part in tail_parts:
+        forward_diagonal(*part)
     for index in range((ring - LAG) // COUNTED, plan.counts - 1):
         first = index * COUNTED
         finish(index, pl.ds(first, min(COUNTED, ring - first)), chunk)

time: 782 us -> 782 us (level)
  no operation moved by 1% of the time
where the time goes in v2:
time: 782 us
  Pallas kernels  758 us (97%)
  waiting for transfers between devices  16.4 us (2%)
    pallas_call x1, Pallas kernels, gather(): pl.pallas_call(functools.partial(gather_kernel, plan), out_shape=[jax.Sha...  635 us
    pallas_call x3, Pallas kernels, place_slabs(): pl.pallas_call(body, in_specs=[hbm] * (1 + len(held)), out_specs=[hbm] *...  89.8 us
    pallas_call x5, Pallas kernels, place_rows(): pl.pallas_call(body, out_shape=[outs[n] for n in made], in_specs=[hbm] *...  32.8 us
    ppermute x14, waiting for transfers between devices, swap(): return lax.ppermute(array, 'dp', [(i, i ^ bit) for i in range(plan.dp)])  16.4 us
  transfers between devices with their start and end apart: 14, of which 5 were waited for; matrix products, arithmetic and copies ran while one was open for 0% of the time, Pallas kernels for 15%

profile of v2, /device:TPU:0, one launch (start us, length us, event | category | flops | bytes accessed | tf_op | source)
XLA Modules:
  0.0 781.6 jit_solution(3870439806378001901)
XLA Ops:
  0.6 634.9 %gather.1 = (bf16[8,31,2176,128]{3,2,1,0:T(8,128)(2,1)}, bf16[960,1024]{1,0:T(8,128)(2,1)}, bf16[960,1024]{1,0:T(8,128)(2,1)}, bf16[16,960,384]{2,1,0:T(8,128)(2...) custom-call(bf16[16,32,1024]{2,1,0:T(8,128)(2,1)} %q.1, ...), custom_call_target="tpu_custom_call" | custom-call | tf_op jit(solution)/shard_map/gather/pallas_call | solution.py:513
  635.5 1.5 collective-permute-start
  637.1 0.6 collective-permute-start.1
  637.7 1.5 collective-permute-start.3
  639.1 0.5 collective-permute-start.4
  639.7 45.5 %shard_map.119 = (bf16[16,768,1024]{2,1,0:T(8,128)(2,1)}, bf16[16,1408,1024]{2,1,0:T(8,128)(2,1)}) custom-call(bf16[8,31,2176,128]{3,2,1,0:T(8,128)(2,1)} %get-tuple-element.56.slab), custom_call_target="tpu_custom_call" | custom-call | flops 10000000 | bytes 142606336 | tf_op jit(solution)/shard_map/pallas_call | solution.py:586
  685.1 0.6 collective-permute-start.6
  685.7 34.0 %shard_map.120.refs_0_ = bf16[37984,1024]{1,0:T(8,128)(2,1)} custom-call(bf16[8,31,2176,128]{3,2,1,0:T(8,128)(2,1)} %get-tuple-element.56.slab), custom_call_target="tpu_custom_call" | custom-call | flops 10000000 | bytes 106954752 | tf_op jit(solution)/shard_map/pallas_call | solution.py:586
  719.7 3.2 collective-permute-done.3.refs_4_
  722.9 1.2 collective-permute-done.4.refs_9_
  724.1 0.5 collective-permute-start.7
  724.6 0.0 collective-permute-start.8
  724.6 0.5 collective-permute-start.9
  725.1 0.6 collective-permute-start.12
  725.7 2.7 collective-permute-done.10.refs_11_
  728.4 0.6 collective-permute-start.2
  729.0 8.9 %shard_map.121 = (bf16[16,704,1024]{2,1,0:T(8,128)(2,1)}, bf16[16,1024,256]{2,1,0:T(8,128)(2,1)}) custom-call(bf16[16,960,384]{2,1,0:T(8,128)(2,1)} %get-tuple-element.53.refs_0_), custom_call_target="tpu_custom_call" | custom-call | flops 10000000 | bytes 23592960 | tf_op jit(solution)/shard_map/pallas_call | solution.py:681
  737.9 10.4 %shard_map.122.refs_14_ = bf16[37984,1024]{1,0:T(8,128)(2,1)} custom-call(bf16[8,31,2176,128]{3,2,1,0:T(8,128)(2,1)} %get-tuple-element.56.slab, bf16[37984,1024]{1,0:T(8,128)(2,1)} %shard_map.120.refs_0_), custom_call_target="tpu_custom_call", output_to_operand_aliasing={{}: (1, {})} | custom-call | flops 10000000 | bytes 26738688 | tf_op jit(solution)/shard_map/pallas_call | solution.py:586
  748.3 15.9 %shard_map.123 = (bf16[16,704,1024]{2,1,0:T(8,128)(2,1)}, bf16[16,1024,256]{2,1,0:T(8,128)(2,1)}, bf16[37984,1024]{1,0:T(8,128)(2,1)}) custom-call(bf16[960,1024]{1,0:T(8,128)(2,1)} %get-tuple-element.58.refs_0_, bf16[960,1024]{1,0:T(8,128)(2,1)} %get-tuple-element.59.refs_1_, ...), custom_call_target="tpu_custom_call", output_to_operand_aliasing={{0}: (12, {}), {1}: (13, {}), {2}: (14, {})} | custom-call | flops 10000000 | bytes 47185920 | tf_op jit(solution)/shard_map/pallas_call | solution.py:681
  764.3 5.9 collective-permute-done.12.refs_0_
  770.2 3.3 collective-permute-done.2.refs_1_
  773.6 3.2 shard_map.124
  776.8 2.4 shard_map.125
  779.2 2.4 shard_map.126
  (13 shorter events, 0.0 us)
Async XLA Ops:
  635.5 49.6 %collective-permute-start = (bf16[960,1024]{1,0:T(8,128)(2,1)}, bf16[960,1024]{1,0:T(8,128)(2,1)}, u32[]{:S(2)}, u32[]{:S(2)}) collective-permute-start(bf16[960,1024]{1,0:T(8,128)(2,1)} %get-tuple-element.59.refs_1_), channel_id=1, source_target_pairs={{0,2},{1,3},{2,0},{3,1},{4,6},{5,7},{6,4},{7,5},{8,10},{9,11},{10,... | collective-permute-start | bytes 5898248 | tf_op jit(solution)/shard_map/ppermute | solution.py:732
  637.1 48.7 %collective-permute-start.1 = (bf16[960,1024]{1,0:T(8,128)(2,1)}, bf16[960,1024]{1,0:T(8,128)(2,1)}, u32[]{:S(2)}, u32[]{:S(2)}) collective-permute-start(bf16[960,1024]{1,0:T(8,128)(2,1)} %get-tuple-element.58.refs_0_), channel_id=1, source_target_pairs={{0,4},{1,5},{2,6},{3,7},{4,0},{5,1},{6,2},{7,3},{8,12},{9,13},{10,... | collective-permute-start | bytes 5898248 | tf_op jit(solution)/shard_map/ppermute | solution.py:732
  637.7 85.3 %collective-permute-start.3 = (bf16[960,1024]{1,0:T(8,128)(2,1)}, bf16[960,1024]{1,0:T(8,128)(2,1)}, u32[]{:S(2)}, u32[]{:S(2)}) collective-permute-start(bf16[960,1024]{1,0:T(8,128)(2,1)} %get-tuple-element.58.refs_0_), channel_id=1, source_target_pairs={{0,2},{1,3},{2,0},{3,1},{4,6},{5,7},{6,4},{7,5},{8,10},{9,11},{10,... | collective-permute-start | bytes 5898248 | tf_op jit(solution)/shard_map/ppermute | solution.py:732
  639.1 84.9 %collective-permute-start.4 = (bf16[960,1024]{1,0:T(8,128)(2,1)}, bf16[960,1024]{1,0:T(8,128)(2,1)}, u32[]{:S(2)}, u32[]{:S(2)}) collective-permute-start(bf16[960,1024]{1,0:T(8,128)(2,1)} %get-tuple-element.59.refs_1_), channel_id=1, source_target_pairs={{0,4},{1,5},{2,6},{3,7},{4,0},{5,1},{6,2},{7,3},{8,12},{9,13},{10,... | collective-permute-start | bytes 5898248 | tf_op jit(solution)/shard_map/ppermute | solution.py:732
  639.7 85.0 %collective-permute-start.5 = (bf16[960,1024]{1,0:T(8,128)(2,1)}, bf16[960,1024]{1,0:T(8,128)(2,1)}, u32[]{:S(2)}, u32[]{:S(2)}) collective-permute-start(bf16[960,1024]{1,0:T(8,128)(2,1)} %get-tuple-element.58.refs_0_), channel_id=1, source_target_pairs={{0,1},{1,0},{2,3},{3,2},{4,5},{5,4},{6,7},{7,6},{8,9},{9,8},{10,11... | collective-permute-start | bytes 5898248 | tf_op jit(solution)/shard_map/ppermute | solution.py:732
  685.1 40.0 %collective-permute-start.6 = (bf16[960,1024]{1,0:T(8,128)(2,1)}, bf16[960,1024]{1,0:T(8,128)(2,1)}, u32[]{:S(2)}, u32[]{:S(2)}) collective-permute-start(bf16[960,1024]{1,0:T(8,128)(2,1)} %get-tuple-element.59.refs_1_), channel_id=1, source_target_pairs={{0,1},{1,0},{2,3},{3,2},{4,5},{5,4},{6,7},{7,6},{8,9},{9,8},{10,11... | collective-permute-start | bytes 5898248 | tf_op jit(solution)/shard_map/ppermute | solution.py:732
  724.1 4.3 collective-permute-start.10
  724.1 24.2 %collective-permute-start.7 = (bf16[960,1024]{1,0:T(8,128)(2,1)}, bf16[960,1024]{1,0:T(8,128)(2,1)}, u32[]{:S(2)}, u32[]{:S(2)}) collective-permute-start(bf16[960,1024]{1,0:T(8,128)(2,1)} %collective-permute-done.3.refs_4_), channel_id=1, source_target_pairs={{0,1},{1,0},{2,3},{3,2},{4,5},{5,4},{6,7},{7,6},{8,9},{9,8},{10,11... | collective-permute-start | bytes 5898248 | tf_op jit(solution)/shard_map/ppermute | solution.py:732
  724.6 23.7 %collective-permute-start.8 = (bf16[960,1024]{1,0:T(8,128)(2,1)}, bf16[960,1024]{1,0:T(8,128)(2,1)}, u32[]{:S(2)}, u32[]{:S(2)}) collective-permute-start(bf16[960,1024]{1,0:T(8,128)(2,1)} %collective-permute-done.refs_5_), channel_id=1, source_target_pairs={{0,1},{1,0},{2,3},{3,2},{4,5},{5,4},{6,7},{7,6},{8,9},{9,8},{10,11... | collective-permute-start | bytes 5898248 | tf_op jit(solution)/shard_map/ppermute | solution.py:732
  724.6 23.7 %collective-permute-start.9 = (bf16[960,1024]{1,0:T(8,128)(2,1)}, bf16[960,1024]{1,0:T(8,128)(2,1)}, u32[]{:S(2)}, u32[]{:S(2)}) collective-permute-start(bf16[960,1024]{1,0:T(8,128)(2,1)} %collective-permute-done.1.refs_8_), channel_id=1, source_target_pairs={{0,1},{1,0},{2,3},{3,2},{4,5},{5,4},{6,7},{7,6},{8,9},{9,8},{10,11... | collective-permute-start | bytes 5898248 | tf_op jit(solution)/shard_map/ppermute | solution.py:732
  725.1 45.1 %collective-permute-start.12 = (bf16[960,1024]{1,0:T(8,128)(2,1)}, bf16[960,1024]{1,0:T(8,128)(2,1)}, u32[]{:S(2)}, u32[]{:S(2)}) collective-permute-start(bf16[960,1024]{1,0:T(8,128)(2,1)} %collective-permute-done.1.refs_8_), channel_id=1, source_target_pairs={{0,2},{1,3},{2,0},{3,1},{4,6},{5,7},{6,4},{7,5},{8,10},{9,11},{10,... | collective-permute-start | bytes 5898248 | tf_op jit(solution)/shard_map/ppermute | solution.py:732
  728.4 45.2 %collective-permute-start.2 = (bf16[960,1024]{1,0:T(8,128)(2,1)}, bf16[960,1024]{1,0:T(8,128)(2,1)}, u32[]{:S(2)}, u32[]{:S(2)}) collective-permute-start(bf16[960,1024]{1,0:T(8,128)(2,1)} %collective-permute-done.refs_5_), channel_id=1, source_target_pairs={{0,4},{1,5},{2,6},{3,7},{4,0},{5,1},{6,2},{7,3},{8,12},{9,13},{10,... | collective-permute-start | bytes 5898248 | tf_op jit(solution)/shard_map/ppermute | solution.py:732
  770.2 6.6 collective-permute-start.13
  773.6 5.6 collective-permute-start.11
